TPU v7x, 32 devices: a whole 2x2x4 slice. The times are simulated.
32 devices in a mesh: grp: 2 (over x), dom: 16 (over z, y, core).
Axes of the slice: x: 2, y: 2, z: 4, core: 2. Of those that a mesh axis runs over, the one named last changes fastest.
Arguments:
- positions: float32 [512, 3, 128], P(('grp', 'dom')), may hold values from 0 to 1
- smoothing: float32 [512, 128], P(('grp', 'dom')), may hold values from 0.35 to 0.55
- energy: float32 [512, 128], P(('grp', 'dom')), may hold values from 0.5 to 2
- mass: float32 [512, 128], P(('grp', 'dom')), may hold values from 0.00390625 to 0.015625
- old_density: float32 [512, 128], P(('grp', 'dom')), may hold values from 1 to 6
- active: int32 [512, 128], P(('grp', 'dom')), may hold values 0 or 1
- pair_list: int32 [512, 2], P(('grp', 'dom')), may hold values from 0 to 15
- export_leaves: int32 [768, 2], P(('grp', 'dom')), may hold values from 0 to 15
- export_route: int32 [768, 1], P(('grp', 'dom')), may hold values from 0 to 14; in each aligned block of 24 rows (0 to 23, 24 to 47, ...) at most 2 rows name the same one
Outputs:
- density: float32 [512, 128], P(('grp', 'dom'))
- acceleration: float32 [512, 3, 128], P(('grp', 'dom'))
- timestep: float32 [], replicated
Inputs may be any that keep to these rules, and one draw needn't show every extreme that they name: `pair_list`: indices of leaf blocks of the domain that holds the row. `export_leaves`: column 0 is a leaf block of the domain that holds the row, column 1 a leaf block of the destination domain. `export_route`: among the rows of one domain no value occurs more than 2 times; in some domains one value occurs exactly 2 times. `active`: every domain holds some particles with value 1.
All inputs are finite; a program needn't handle non-finite values. No bound on the sum of `active` on one device may be relied on, other than what follows from the above.
Results may differ from a plain program's by a relative error of at most 0.0003.
Values sent between devices are 32-bit elements; how exact they have to be, the bound alone decides.
No kernel may reach another device: no remote copies, remote signals or barrier semaphores. Data moves between devices by JAX's collectives and lax.ppermute only.
A program may use at most 64 MiB of HBM per device.

v0:
```python
import math
import jax
import jax.numpy as jnp
from jax import lax
from jax.sharding import PartitionSpec as P

MOST = 2
ADIABATIC = 5.0 / 3.0
COURANT = 0.3
batch_tiles = 8


def kernel_value(dist, smooth):
    ratio = dist / smooth
    inner = 1.0 - 6.0 * ratio * ratio + 6.0 * ratio * ratio * ratio
    remain = jnp.maximum(1.0 - ratio, 0.0)
    outer = 2.0 * remain * remain * remain
    return jnp.where(ratio < 0.5, inner, outer) * (8.0 / math.pi) / (smooth * smooth * smooth)


def kernel_slope(dist, smooth):
    ratio = dist / smooth
    inner = -12.0 + 18.0 * ratio
    remain = jnp.maximum(1.0 - ratio, 0.0)
    outer = -6.0 * remain * remain / jnp.maximum(ratio, 0.5)
    square = smooth * smooth
    return jnp.where(ratio < 0.5, inner, outer) * (8.0 / math.pi) / (square * square * smooth)


def density_tile(own_pos, own_h, far_pos, far_mass):
    offset = own_pos[:, :, None] - far_pos[:, None, :]
    dist = jnp.sqrt(jnp.sum(offset * offset, axis=0))
    return jnp.sum(kernel_value(dist, own_h[:, None]) * far_mass[None, :], axis=1)


def force_tile(own_pos, own_h, own_term, far_pos, far_h, far_mass, far_term):
    offset = own_pos[:, :, None] - far_pos[:, None, :]
    dist = jnp.sqrt(jnp.sum(offset * offset, axis=0))
    slope = 0.5 * (kernel_slope(dist, own_h[:, None]) + kernel_slope(dist, far_h[None, :]))
    weight = far_mass[None, :] * (own_term[:, None] + far_term[None, :]) * slope
    return -jnp.sum(weight[None, :, :] * offset, axis=2)


def blockwise(kernel, operands):
    count = operands[0].shape[0]
    width = min(batch_tiles, count)
    shaped = tuple((item.reshape((count // width, width) + item.shape[1:]) for item in operands))
    result = lax.map(lambda group: jax.vmap(kernel)(*group), shaped)
    return result.reshape((count,) + result.shape[2:])


def collect(owner, values):
    flat = values.reshape(values.shape[0], -1)
    total = jnp.dot(
        owner, flat, precision=lax.Precision.HIGHEST, preferred_element_type=jnp.float32
    )
    return total.reshape((owner.shape[0],) + values.shape[1:])


def body(
    positions, smoothing, energy, mass, old_density, active, pair_list, export_leaves, export_route
):
    leaves = positions.shape[0]
    width = positions.shape[2]
    exported = export_leaves.shape[0]
    domains = lax.axis_size("dom")
    myself = lax.axis_index("dom")
    slots = domains * MOST
    target_dom = (myself + 1 + export_route[:, 0]) % domains
    columns = jnp.arange(domains, dtype=jnp.int32)
    onehot = (target_dom[:, None] == columns[None, :]).astype(jnp.int32)
    earlier = jnp.cumsum(onehot, axis=0) - onehot
    rank_in = jnp.sum(earlier * onehot, axis=1)
    slot_of = target_dom * MOST + rank_in
    match = (slot_of[None, :] == jnp.arange(slots, dtype=jnp.int32)[:, None]).astype(jnp.int32)
    filled = jnp.sum(match, axis=1) > 0
    chosen = jnp.sum(match * jnp.arange(exported, dtype=jnp.int32)[None, :], axis=1)
    send_leaf = export_leaves[chosen, 0]
    send_target = jnp.where(filled, export_leaves[chosen, 1], 0)
    leaf_ids = jnp.arange(leaves, dtype=jnp.int32)
    slot_owner = ((send_leaf[None, :] == leaf_ids[:, None]) & filled[None, :]).astype(jnp.float32)
    pair_owner = (pair_list[None, :, 0] == leaf_ids[:, None]).astype(jnp.float32)
    own_idx = pair_list[:, 0]
    far_idx = pair_list[:, 1]
    send_pos = positions[send_leaf]
    send_h = smoothing[send_leaf]
    wanted = lax.all_to_all(
        send_target.reshape(domains, MOST), "dom", split_axis=0, concat_axis=0, tiled=True
    )
    wanted = wanted.reshape(slots)
    served = jnp.concatenate(
        [positions[wanted], smoothing[wanted][:, None, :], mass[wanted][:, None, :]], axis=1
    )
    fetched = lax.all_to_all(
        served.reshape(domains, MOST, 5, width), "dom", split_axis=0, concat_axis=0, tiled=True
    )
    fetched = fetched.reshape(slots, 5, width)
    remote_density = collect(
        slot_owner, blockwise(density_tile, (send_pos, send_h, fetched[:, 0:3], fetched[:, 4]))
    )
    local_part = blockwise(
        density_tile, (positions[own_idx], smoothing[own_idx], positions[far_idx], mass[far_idx])
    )
    self_term = mass * kernel_value(jnp.zeros_like(smoothing), smoothing)
    summed = collect(pair_owner, local_part) + remote_density
    density = jnp.where(active == 1, self_term + summed, old_density)
    term = (ADIABATIC - 1.0) * energy / density
    far_term = lax.all_to_all(
        term[wanted].reshape(domains, MOST, width), "dom", split_axis=0, concat_axis=0, tiled=True
    )
    far_term = far_term.reshape(slots, width)
    remote_force = blockwise(
        force_tile,
        (
            send_pos,
            send_h,
            term[send_leaf],
            fetched[:, 0:3],
            fetched[:, 3],
            fetched[:, 4],
            far_term,
        ),
    )
    remote_accel = collect(slot_owner, remote_force)
    local_force = blockwise(
        force_tile,
        (
            positions[own_idx],
            smoothing[own_idx],
            term[own_idx],
            positions[far_idx],
            smoothing[far_idx],
            mass[far_idx],
            term[far_idx],
        ),
    )
    accel = collect(pair_owner, local_force) + remote_accel
    acceleration = jnp.where((active == 1)[:, None, :], accel, 0.0)
    speed = jnp.sqrt(ADIABATIC * (ADIABATIC - 1.0) * energy)
    magnitude = jnp.sqrt(jnp.sum(acceleration * acceleration, axis=1))
    step_size = COURANT * smoothing / (speed + jnp.sqrt(smoothing * magnitude))
    local_least = jnp.min(jnp.where(active == 1, step_size, jnp.inf))
    timestep = lax.pmin(local_least, ("grp", "dom"))
    return (density, acceleration, timestep)


def solution(mesh):
    return jax.shard_map(
        body,
        mesh=mesh,
        in_specs=(
            P(("grp", "dom"), None, None),
            P(("grp", "dom"), None),
            P(("grp", "dom"), None),
            P(("grp", "dom"), None),
            P(("grp", "dom"), None),
            P(("grp", "dom"), None),
            P(("grp", "dom"), None),
            P(("grp", "dom"), None),
            P(("grp", "dom"), None),
        ),
        out_specs=(P(("grp", "dom"), None), P(("grp", "dom"), None, None), P()),
        check_vma=False,
    )
```

profile of v0, /device:TPU:0, one launch (start us, length us, event | category | flops | bytes accessed | tf_op | source)
XLA Modules:
  0.0 107.7 jit_solution(8637589466511635926)
XLA Ops:
  2.4 1.4 %gather_fusion.6 = s32[32]{0:T(128)S(1)} fusion(s32[24,2]{0,1:T(2,128)} %param.24, s32[32]{0:T(128)S(1)} %get-tuple-element.380), kind=kCustom, calls=%fused_computation.6 | custom fusion | bytes 512 | tf_op jit(solution)/shard_map/gather | solution.py:79
  4.6 7.4 %all-to-all-start = ((s32[16,1,2]{2,1,0:T(1,128)}), s32[16,1,2]{2,1,0:T(1,128)S(1)}, u32[]{:S(2)}, u32[]{:S(2)}) async-start(s32[16,1,2]{2,1,0:T(1,128)} %bitcast.42), calls=%async_computation | async-start | bytes 16384 | tf_op jit(solution)/shard_map/all_to_all | solution.py:87
  17.0 2.3 %while.40 = (s32[]{:T(128)}, f32[2,8,128]{2,1,0:T(8,128)S(1)}, f32[2,8,3,128]{3,2,1,0:T(4,128)S(1)}, f32[2,8,3,128]{3,2,1,0:T(4,128)S(1)}, f32[2,8,128]{2,1,0:T(8,128)S(1)}, /*index=5*/f32[2,8,128]{2,1,0:T(8,128)S(1)}, s32[]{:T(128)}) while((s32[]{:T(128)}, f32[2,8,128]{2,1,0:T(8,128)S(1)}, f32[2,8,3,128]{3,2,1,0:T(4,128)S(1)}, ...), condition=%wide.region_3.4_spmd, body=%wide.region_0.0_spmd.sunk | while | flops 3277826 | bytes 1167461 | solution.py:48
  23.2 6.0 %all-to-all-start.1 = ((f32[16,2,5,128]{3,1,2,0:T(2,128)}), f32[16,2,5,128]{3,1,2,0:T(2,128)S(1)}, u32[]{:S(2)}, u32[]{:S(2)}) async-start(f32[16,2,5,128]{3,1,2,0:T(2,128)} %pad_maximum_fusion), calls=%async_computation.1 | async-start | bytes 163840 | tf_op jit(solution)/shard_map/all_to_all | solution.py:94
  29.3 7.1 %all-to-all-done.1 = f32[16,2,5,128]{3,1,2,0:T(2,128)S(1)} async-done(((f32[16,2,5,128]{3,1,2,0:T(2,128)}), f32[16,2,5,128]{3,1,2,0:T(2,128)S(1)}, u32[]{:S(2)}, u32[]{:S(2)}) %all-to-all-start.1) | async-done | bytes 81952 | tf_op jit(solution)/shard_map/all_to_all | solution.py:94
  36.5 4.6 %while.41 = (s32[]{:T(128)}, f32[4,8,128]{2,1,0:T(8,128)S(1)}, f32[4,8,3,128]{3,2,1,0:T(4,128)S(1)}, f32[4,8,3,128]{3,2,1,0:T(4,128)S(1)}, f32[4,8,128]{2,1,0:T(8,128)S(1)}, /*index=5*/f32[4,8,128]{2,1,0:T(8,128)S(1)}, s32[]{:T(128)}) while((s32[]{:T(128)}, f32[4,8,128]{2,1,0:T(8,128)S(1)}, f32[4,8,3,128]{3,2,1,0:T(4,128)S(1)}, ...), condition=%wide.region_11.12_spmd, body=%wide.region_8.11_spmd.sunk | while | flops 3277826 | bytes 1167461 | solution.py:48
  42.9 1.2 %gather_fusion.15 = f32[32,128]{1,0:T(8,128)} fusion(f32[16,128]{1,0:T(8,128)S(1)} %get-tuple-element.382, s32[1024]{0:T(1024)S(1)} %pad_clamp_fusion), kind=kCustom, calls=%fused_computation.15 | custom fusion | bytes 32896 | tf_op jit(solution)/shard_map/gather | solution.py:109
  44.1 4.6 %while.42 = (s32[]{:T(128)}, f32[2,8,3,128]{3,2,1,0:T(4,128)S(1)}, f32[2,8,128]{2,1,0:T(8,128)S(1)}, f32[2,8,128]{2,1,0:T(8,128)S(1)}, f32[2,8,128]{2,1,0:T(8,12...) while((s32[]{:T(128)}, f32[2,8,3,128]{3,2,1,0:T(4,128)S(1)}, ...), condition=%wide.region_15.16_spmd, body=%wide.region_12.15_spmd.sunk | while | flops 6297602 | bytes 2318465 | solution.py:48
  44.7 0.8 multiply_multiply_fusion.28
  45.4 1.0 fusion.91
  47.0 0.8 multiply_multiply_fusion.28
  47.8 1.0 fusion.91
  48.7 3.5 %all-to-all-start.2 = ((f32[16,2,128]{2,1,0:T(2,128)}), f32[16,2,128]{2,1,0:T(2,128)S(1)}, u32[]{:S(2)}, u32[]{:S(2)}) async-start(f32[16,2,128]{2,1,0:T(2,128)} %bitcast.61), calls=%async_computation.2 | async-start | bytes 32768 | tf_op jit(solution)/shard_map/all_to_all | solution.py:108
  53.0 5.8 %all-to-all-done.2 = f32[16,2,128]{2,1,0:T(2,128)S(1)} async-done(((f32[16,2,128]{2,1,0:T(2,128)}), f32[16,2,128]{2,1,0:T(2,128)S(1)}, u32[]{:S(2)}, u32[]{:S(2)}) %all-to-all-start.2) | async-done | bytes 16416 | tf_op jit(solution)/shard_map/all_to_all | solution.py:108
  58.7 9.3 %while.43 = (s32[]{:T(128)}, f32[4,8,3,128]{3,2,1,0:T(4,128)S(1)}, f32[4,8,128]{2,1,0:T(8,128)S(1)}, f32[4,8,128]{2,1,0:T(8,128)S(1)}, f32[4,8,128]{2,1,0:T(8,12...) while((s32[]{:T(128)}, f32[4,8,3,128]{3,2,1,0:T(4,128)S(1)}, ...), condition=%wide.region_19.20_spmd, body=%wide.region_16.19_spmd.sunk | while | flops 6297602 | bytes 2318465 | solution.py:48
  59.3 0.8 multiply_multiply_fusion.30
  60.1 1.0 fusion.93
  61.6 0.8 multiply_multiply_fusion.30
  62.4 1.0 fusion.93
  63.9 0.8 multiply_multiply_fusion.30
  64.7 1.0 fusion.93
  66.3 0.8 multiply_multiply_fusion.30
  67.0 1.0 fusion.93
  69.4 38.3 %pmin.7 = f32[]{:T(128)} all-reduce(f32[]{:T(128)} %select_reduce_fusion.2), channel_id=1, replica_groups=mesh['grp'=2,'dom'=16] {'grp','dom'}, use_global_device_ids=true, to_apply=%region_22.23 | all-reduce | flops 1 | bytes 8 | tf_op jit(solution)/shard_map/pmin | solution.py:143
  (140 shorter events, 25.0 us)
Async XLA Ops:
  0.6 11.4 %copy-start = (f32[16,3,128]{2,0,1:T(8,128)S(1)}, f32[16,3,128]{2,0,1:T(8,128)}, u32[]{:S(2)}) copy-start(f32[16,3,128]{2,0,1:T(8,128)} %param.17) | copy-start | bytes 73732
  0.6 12.6 %copy-start.1 = (s32[24,2]{0,1:T(2,128)S(1)}, s32[24,2]{0,1:T(2,128)}, u32[]{:S(2)}) copy-start(s32[24,2]{0,1:T(2,128)} %param.24) | copy-start | bytes 580
  0.7 11.4 %copy-start.6 = (s32[16,2]{0,1:T(2,128)S(1)}, s32[16,2]{0,1:T(2,128)}, u32[]{:S(2)}) copy-start(s32[16,2]{0,1:T(2,128)} %param.23) | copy-start | bytes 388
  0.7 12.0 %copy-start.2 = (f32[16,128]{1,0:T(8,128)S(1)}, f32[16,128]{1,0:T(8,128)}, u32[]{:S(2)}) copy-start(f32[16,128]{1,0:T(8,128)} %param.18) | copy-start | bytes 24580
  4.6 14.9 %all-to-all-start = ((s32[16,1,2]{2,1,0:T(1,128)}), s32[16,1,2]{2,1,0:T(1,128)S(1)}, u32[]{:S(2)}, u32[]{:S(2)}) async-start(s32[16,1,2]{2,1,0:T(1,128)} %bitcast.42), calls=%async_computation | async-start | bytes 16384 | tf_op jit(solution)/shard_map/all_to_all | solution.py:87
  14.0 2.4 %copy-start.4 = (s32[16,128]{1,0:T(8,128)S(1)}, s32[16,128]{1,0:T(8,128)}, u32[]{:S(2)}) copy-start(s32[16,128]{1,0:T(8,128)} %param.22) | copy-start | bytes 24580
  14.0 2.4 %copy-start.3 = (f32[16,128]{1,0:T(8,128)S(1)}, f32[16,128]{1,0:T(8,128)}, u32[]{:S(2)}) copy-start(f32[16,128]{1,0:T(8,128)} %param.20) | copy-start | bytes 24580
  23.2 13.1 %all-to-all-start.1 = ((f32[16,2,5,128]{3,1,2,0:T(2,128)}), f32[16,2,5,128]{3,1,2,0:T(2,128)S(1)}, u32[]{:S(2)}, u32[]{:S(2)}) async-start(f32[16,2,5,128]{3,1,2,0:T(2,128)} %pad_maximum_fusion), calls=%async_computation.1 | async-start | bytes 163840 | tf_op jit(solution)/shard_map/all_to_all | solution.py:94
  36.5 4.6 %copy-start.5 = (f32[16,128]{1,0:T(8,128)S(1)}, f32[16,128]{1,0:T(8,128)}, u32[]{:S(2)}) copy-start(f32[16,128]{1,0:T(8,128)} %param.19) | copy-start | bytes 24580
  36.5 4.6 %copy-start.7 = (f32[16,128]{1,0:T(8,128)S(1)}, f32[16,128]{1,0:T(8,128)}, u32[]{:S(2)}) copy-start(f32[16,128]{1,0:T(8,128)} %param.21) | copy-start | bytes 24580
  48.7 10.0 %all-to-all-start.2 = ((f32[16,2,128]{2,1,0:T(2,128)}), f32[16,2,128]{2,1,0:T(2,128)S(1)}, u32[]{:S(2)}, u32[]{:S(2)}) async-start(f32[16,2,128]{2,1,0:T(2,128)} %bitcast.61), calls=%async_computation.2 | async-start | bytes 32768 | tf_op jit(solution)/shard_map/all_to_all | solution.py:108
where the time goes:
time: 108 us
  blocking collectives  38.3 us (35%)
  other arithmetic  23.5 us (22%)
  starting transfers between devices  16.9 us (16%)
  waiting for transfers between devices  12.9 us (12%)
  local copies, waits for them, and re-layouts  12.7 us (12%)
  matrix products  1.74 us (2%)
    pmin x1, blocking collectives, body(): timestep = lax.pmin(local_least, ('grp', 'dom'))  38.3 us
    all_to_all x1, starting transfers between devices, body(): lax.all_to_all(send_target.reshape(domains, MOST), 'dom', split_axis=0, c...  7.41 us
    all_to_all x1, waiting for transfers between devices, body(): lax.all_to_all(served.reshape(domains, MOST, 5, width), 'dom', split_axis...  7.1 us
    all_to_all x1, starting transfers between devices, body(): lax.all_to_all(served.reshape(domains, MOST, 5, width), 'dom', split_axis...  6 us
    all_to_all x1, waiting for transfers between devices, body(): lax.all_to_all(term[wanted].reshape(domains, MOST, width), 'dom', split_a...  5.75 us
    reduce_sum x6, other arithmetic, force_tile(): return -jnp.sum(weight[None, :, :] * offset, axis=2)  5.74 us
    mul x6, other arithmetic, force_tile(): weight = far_mass[None, :] * (own_term[:, None] + far_term[None, :]) * slope  4.61 us
    all_to_all x1, starting transfers between devices, body(): lax.all_to_all(term[wanted].reshape(domains, MOST, width), 'dom', split_a...  3.51 us
  transfers between devices with their start and end apart: 3, of which 2 were waited for; matrix products, arithmetic and copies ran while one was open for 7% of the time, Pallas kernels for 0%

commit v1 on v0

--- a/solution.py
+++ b/solution.py
@@ -8,6 +8,18 @@
 ADIABATIC = 5.0 / 3.0
 COURANT = 0.3
 batch_tiles = 8
+
+
+def sent_to_each(shard, axis, split, join):
+    ways, here = (lax.axis_size(axis), lax.axis_index(axis))
+    width = shard.shape[split] // ways
+    turned = jnp.roll(shard, -here * width, axis=split)
+    got = [lax.slice_in_dim(turned, 0, width, axis=split)]
+    for far in range(1, ways):
+        sent = lax.slice_in_dim(turned, far * width, (far + 1) * width, axis=split)
+        got.append(lax.ppermute(sent, axis, [(d, (d + far) % ways) for d in range(ways)]))
+    line = jnp.concatenate(got[::-1], axis=join)
+    return jnp.roll(line, (here + 1) * got[0].shape[join], axis=join)
 
 
 def kernel_value(dist, smooth):
@@ -91,9 +103,7 @@
     served = jnp.concatenate(
         [positions[wanted], smoothing[wanted][:, None, :], mass[wanted][:, None, :]], axis=1
     )
-    fetched = lax.all_to_all(
-        served.reshape(domains, MOST, 5, width), "dom", split_axis=0, concat_axis=0, tiled=True
-    )
+    fetched = sent_to_each(served.reshape(domains, MOST, 5, width), "dom", 0, 0)
     fetched = fetched.reshape(slots, 5, width)
     remote_density = collect(
         slot_owner, blockwise(density_tile, (send_pos, send_h, fetched[:, 0:3], fetched[:, 4]))

time: 108 us -> 121 us (1.12)
  starting transfers between devices: 16.9 us -> 31.7 us
  waiting for transfers between devices: 12.9 us -> 11.5 us
    ppermute x0 -> x15, starting transfers between devices: none -> 20.8 us  [sent_to_each(): lax.ppermute(sent, axis, [(d, (d + far) % ways) for d in range(ways)])]
    all_to_all x1 -> x0, waiting for transfers between devices: 7.1 us -> none  [body(): lax.all_to_all(served.reshape(domains, MOST, 5, width), 'dom', split_axis...]
    all_to_all x1 -> x0, starting transfers between devices: 6 us -> none  [body(): lax.all_to_all(served.reshape(domains, MOST, 5, width), 'dom', split_axis...]
    ppermute x0 -> x15, waiting for transfers between devices: none -> 5.7 us  [sent_to_each(): lax.ppermute(sent, axis, [(d, (d + far) % ways) for d in range(ways)])]
  transfers between devices with their start and end apart: 3 -> 17, of which waited for: 2 -> 6; matrix products, arithmetic and copies ran while one was open for 7% -> 7% of each run, Pallas kernels for 0% -> 0%
where the time goes in v1:
time: 121 us
  blocking collectives  38.3 us (32%)
  starting transfers between devices  31.7 us (26%)
  other arithmetic  23 us (19%)
  local copies, waits for them, and re-layouts  12.9 us (11%)
  waiting for transfers between devices  11.5 us (10%)
  matrix products  1.74 us (1%)
    pmin x1, blocking collectives, body(): timestep = lax.pmin(local_least, ('grp', 'dom'))  38.3 us
    ppermute x15, starting transfers between devices, sent_to_each(): lax.ppermute(sent, axis, [(d, (d + far) % ways) for d in range(ways)])  20.8 us
    all_to_all x1, starting transfers between devices, body(): lax.all_to_all(send_target.reshape(domains, MOST), 'dom', split_axis=0, c...  7.41 us
    all_to_all x1, waiting for transfers between devices, body(): lax.all_to_all(term[wanted].reshape(domains, MOST, width), 'dom', split_a...  5.75 us
    reduce_sum x6, other arithmetic, force_tile(): return -jnp.sum(weight[None, :, :] * offset, axis=2)  5.74 us
    ppermute x15, waiting for transfers between devices, sent_to_each(): lax.ppermute(sent, axis, [(d, (d + far) % ways) for d in range(ways)])  5.7 us
    mul x6, other arithmetic, force_tile(): weight = far_mass[None, :] * (own_term[:, None] + far_term[None, :]) * slope  4.61 us
    all_to_all x1, starting transfers between devices, body(): lax.all_to_all(term[wanted].reshape(domains, MOST, width), 'dom', split_a...  3.51 us
  transfers between devices with their start and end apart: 17, of which 6 were waited for; matrix products, arithmetic and copies ran while one was open for 7% of the time, Pallas kernels for 0%

profile of v1, /device:TPU:0, one launch (start us, length us, event | category | flops | bytes accessed | tf_op | source)
XLA Modules:
  0.0 121.0 jit_solution(3737744499724833655)
XLA Ops:
  2.4 1.4 %gather_fusion.6 = s32[32]{0:T(128)S(1)} fusion(s32[24,2]{0,1:T(2,128)} %param.26, s32[32]{0:T(128)S(1)} %get-tuple-element.366), kind=kCustom, calls=%fused_computation.6 | custom fusion | bytes 512 | tf_op jit(solution)/shard_map/gather | solution.py:91
  4.6 7.4 %all-to-all-start = ((s32[16,1,2]{2,1,0:T(1,128)}), s32[16,1,2]{2,1,0:T(1,128)S(1)}, u32[]{:S(2)}, u32[]{:S(2)}) async-start(s32[16,1,2]{2,1,0:T(1,128)} %bitcast.42), calls=%async_computation | async-start | bytes 16384 | tf_op jit(solution)/shard_map/all_to_all | solution.py:99
  15.1 2.3 %while.40 = (s32[]{:T(128)}, f32[2,8,128]{2,1,0:T(8,128)S(1)}, f32[2,8,3,128]{3,2,1,0:T(4,128)S(1)}, f32[2,8,3,128]{3,2,1,0:T(4,128)S(1)}, f32[2,8,128]{2,1,0:T(8,128)S(1)}, /*index=5*/f32[2,8,128]{2,1,0:T(8,128)S(1)}, s32[]{:T(128)}) while((s32[]{:T(128)}, f32[2,8,128]{2,1,0:T(8,128)S(1)}, f32[2,8,3,128]{3,2,1,0:T(4,128)S(1)}, ...), condition=%wide.region_3.4_spmd, body=%wide.region_0.0_spmd.sunk | while | flops 3277826 | bytes 1167461 | solution.py:60
  21.6 4.3 %collective-permute-start = (f32[1,2,5,128]{3,1,0,2:T(2,128)S(1)}, f32[1,2,5,128]{3,1,0,2:T(2,128)S(1)}, u32[]{:S(2)}, u32[]{:S(2)}) collective-permute-start(f32[1,2,5,128]{3,1,0,2:T(2,128)S(1)} %get-tuple-element.362), channel_id=1, source_target_pairs={{0,15},{1,0},{2,1},{3,2},{4,3},{5,4},{6,5},{7,6},{8,7},{9,8},{10,9... | collective-permute-start | bytes 15368 | tf_op jit(solution)/shard_map/ppermute | solution.py:20
  28.8 4.3 %collective-permute-start.5 = (f32[1,2,5,128]{3,1,0,2:T(2,128)S(1)}, f32[1,2,5,128]{3,1,0,2:T(2,128)S(1)}, u32[]{:S(2)}, u32[]{:S(2)}) collective-permute-start(f32[1,2,5,128]{3,1,0,2:T(2,128)S(1)} %get-tuple-element.357), channel_id=1, source_target_pairs={{0,10},{1,11},{2,12},{3,13},{4,14},{5,15},{6,0},{7,1},{8,2},{9,3},... | collective-permute-start | bytes 15368 | tf_op jit(solution)/shard_map/ppermute | solution.py:20
  33.1 1.4 %collective-permute-start.7 = (f32[1,2,5,128]{3,1,0,2:T(2,128)S(1)}, f32[1,2,5,128]{3,1,0,2:T(2,128)S(1)}, u32[]{:S(2)}, u32[]{:S(2)}) collective-permute-start(f32[1,2,5,128]{3,1,0,2:T(2,128)S(1)} %get-tuple-element.355), channel_id=1, source_target_pairs={{0,8},{1,9},{2,10},{3,11},{4,12},{5,13},{6,14},{7,15},{8,0},{9,1},... | collective-permute-start | bytes 15368 | tf_op jit(solution)/shard_map/ppermute | solution.py:20
  34.6 1.5 %collective-permute-start.8 = (f32[1,2,5,128]{3,1,0,2:T(2,128)S(1)}, f32[1,2,5,128]{3,1,0,2:T(2,128)S(1)}, u32[]{:S(2)}, u32[]{:S(2)}) collective-permute-start(f32[1,2,5,128]{3,1,0,2:T(2,128)S(1)} %get-tuple-element.354), channel_id=1, source_target_pairs={{0,7},{1,8},{2,9},{3,10},{4,11},{5,12},{6,13},{7,14},{8,15},{9,0},... | collective-permute-start | bytes 15368 | tf_op jit(solution)/shard_map/ppermute | solution.py:20
  36.1 2.4 %collective-permute-start.9 = (f32[1,2,5,128]{3,1,0,2:T(2,128)S(1)}, f32[1,2,5,128]{3,1,0,2:T(2,128)S(1)}, u32[]{:S(2)}, u32[]{:S(2)}) collective-permute-start(f32[1,2,5,128]{3,1,0,2:T(2,128)S(1)} %get-tuple-element.353), channel_id=1, source_target_pairs={{0,6},{1,7},{2,8},{3,9},{4,10},{5,11},{6,12},{7,13},{8,14},{9,15},... | collective-permute-start | bytes 15368 | tf_op jit(solution)/shard_map/ppermute | solution.py:20
  38.6 2.3 %collective-permute-start.11 = (f32[1,2,5,128]{3,1,0,2:T(2,128)S(1)}, f32[1,2,5,128]{3,1,0,2:T(2,128)S(1)}, u32[]{:S(2)}, u32[]{:S(2)}) collective-permute-start(f32[1,2,5,128]{3,1,0,2:T(2,128)S(1)} %get-tuple-element.351), channel_id=1, source_target_pairs={{0,4},{1,5},{2,6},{3,7},{4,8},{5,9},{6,10},{7,11},{8,12},{9,13},{1... | collective-permute-start | bytes 15368 | tf_op jit(solution)/shard_map/ppermute | solution.py:20
  40.9 2.1 %collective-permute-start.12 = (f32[1,2,5,128]{3,1,0,2:T(2,128)S(1)}, f32[1,2,5,128]{3,1,0,2:T(2,128)S(1)}, u32[]{:S(2)}, u32[]{:S(2)}) collective-permute-start(f32[1,2,5,128]{3,1,0,2:T(2,128)S(1)} %get-tuple-element.350), channel_id=1, source_target_pairs={{0,3},{1,4},{2,5},{3,6},{4,7},{5,8},{6,9},{7,10},{8,11},{9,12},{10... | collective-permute-start | bytes 15368 | tf_op jit(solution)/shard_map/ppermute | solution.py:20
  44.0 2.3 %collective-permute-done.12 = f32[1,2,5,128]{3,1,0,2:T(2,128)S(1)} collective-permute-done((f32[1,2,5,128]{3,1,0,2:T(2,128)S(1)}, f32[1,2,5,128]{3,1,0,2:T(2,128)S(1)}, u32[]{:S(2)}, u32[]{:S(2)}) %collective-permute-start.12) | collective-permute-done | bytes 5152 | tf_op jit(solution)/shard_map/ppermute | solution.py:20
  46.4 3.0 %collective-permute-done.13 = f32[1,2,5,128]{3,1,0,2:T(2,128)S(1)} collective-permute-done((f32[1,2,5,128]{3,1,0,2:T(2,128)S(1)}, f32[1,2,5,128]{3,1,0,2:T(2,128)S(1)}, u32[]{:S(2)}, u32[]{:S(2)}) %collective-permute-start.13) | collective-permute-done | bytes 5152 | tf_op jit(solution)/shard_map/ppermute | solution.py:20
  49.8 4.6 %while.41 = (s32[]{:T(128)}, f32[4,8,128]{2,1,0:T(8,128)S(1)}, f32[4,8,3,128]{3,2,1,0:T(4,128)S(1)}, f32[4,8,3,128]{3,2,1,0:T(4,128)S(1)}, f32[4,8,128]{2,1,0:T(8,128)S(1)}, /*index=5*/f32[4,8,128]{2,1,0:T(8,128)S(1)}, s32[]{:T(128)}) while((s32[]{:T(128)}, f32[4,8,128]{2,1,0:T(8,128)S(1)}, f32[4,8,3,128]{3,2,1,0:T(4,128)S(1)}, ...), condition=%wide.region_11.13_spmd, body=%wide.region_8.12_spmd.sunk | while | flops 3277826 | bytes 1167461 | solution.py:60
  56.2 1.2 gather_fusion.15
  57.4 4.6 %while.42 = (s32[]{:T(128)}, f32[2,8,3,128]{3,2,1,0:T(4,128)S(1)}, f32[2,8,128]{2,1,0:T(8,128)S(1)}, f32[2,8,128]{2,1,0:T(8,128)S(1)}, f32[2,8,128]{2,1,0:T(8,12...) while((s32[]{:T(128)}, f32[2,8,3,128]{3,2,1,0:T(4,128)S(1)}, ...), condition=%wide.region_15.17_spmd, body=%wide.region_12.16_spmd.sunk | while | flops 6297602 | bytes 2318465 | solution.py:60
  58.7 1.0 fusion.97
  62.0 3.5 %all-to-all-start.1 = ((f32[16,2,128]{2,1,0:T(2,128)}), f32[16,2,128]{2,1,0:T(2,128)S(1)}, u32[]{:S(2)}, u32[]{:S(2)}) async-start(f32[16,2,128]{2,1,0:T(2,128)} %bitcast.59), calls=%async_computation.1 | async-start | bytes 32768 | tf_op jit(solution)/shard_map/all_to_all | solution.py:118
  66.2 5.8 %all-to-all-done.1 = f32[16,2,128]{2,1,0:T(2,128)S(1)} async-done(((f32[16,2,128]{2,1,0:T(2,128)}), f32[16,2,128]{2,1,0:T(2,128)S(1)}, u32[]{:S(2)}, u32[]{:S(2)}) %all-to-all-start.1) | async-done | bytes 16416 | tf_op jit(solution)/shard_map/all_to_all | solution.py:118
  72.0 9.3 %while.43 = (s32[]{:T(128)}, f32[4,8,3,128]{3,2,1,0:T(4,128)S(1)}, f32[4,8,128]{2,1,0:T(8,128)S(1)}, f32[4,8,128]{2,1,0:T(8,128)S(1)}, f32[4,8,128]{2,1,0:T(8,12...) while((s32[]{:T(128)}, f32[4,8,3,128]{3,2,1,0:T(4,128)S(1)}, ...), condition=%wide.region_19.21_spmd, body=%wide.region_16.20_spmd.sunk | while | flops 6297602 | bytes 2318465 | solution.py:60
  73.3 1.0 fusion.99
  75.6 1.0 fusion.99
  78.0 1.0 fusion.99
  80.3 1.0 fusion.99
  82.7 38.3 %pmin.7 = f32[]{:T(128)} all-reduce(f32[]{:T(128)} %select_reduce_fusion.2), channel_id=1, replica_groups=mesh['grp'=2,'dom'=16] {'grp','dom'}, use_global_device_ids=true, to_apply=%region_22.24 | all-reduce | flops 1 | bytes 8 | tf_op jit(solution)/shard_map/pmin | solution.py:153
  (184 shorter events, 33.2 us)
Async XLA Ops:
  0.6 11.5 %copy-start = (f32[16,3,128]{2,0,1:T(8,128)S(1)}, f32[16,3,128]{2,0,1:T(8,128)}, u32[]{:S(2)}) copy-start(f32[16,3,128]{2,0,1:T(8,128)} %param.19) | copy-start | bytes 73732
  0.6 11.4 %copy-start.6 = (s32[16,2]{0,1:T(2,128)S(1)}, s32[16,2]{0,1:T(2,128)}, u32[]{:S(2)}) copy-start(s32[16,2]{0,1:T(2,128)} %param.25) | copy-start | bytes 388
  2.4 10.9 %copy-start.2 = (f32[16,128]{1,0:T(8,128)S(1)}, f32[16,128]{1,0:T(8,128)}, u32[]{:S(2)}) copy-start(f32[16,128]{1,0:T(8,128)} %param.20) | copy-start | bytes 24580
  3.9 10.6 %copy-start.4 = (s32[16,128]{1,0:T(8,128)S(1)}, s32[16,128]{1,0:T(8,128)}, u32[]{:S(2)}) copy-start(s32[16,128]{1,0:T(8,128)} %param.24) | copy-start | bytes 24580
  3.9 10.6 %copy-start.3 = (f32[16,128]{1,0:T(8,128)S(1)}, f32[16,128]{1,0:T(8,128)}, u32[]{:S(2)}) copy-start(f32[16,128]{1,0:T(8,128)} %param.22) | copy-start | bytes 24580
  4.6 13.8 %all-to-all-start = ((s32[16,1,2]{2,1,0:T(1,128)}), s32[16,1,2]{2,1,0:T(1,128)S(1)}, u32[]{:S(2)}, u32[]{:S(2)}) async-start(s32[16,1,2]{2,1,0:T(1,128)} %bitcast.42), calls=%async_computation | async-start | bytes 16384 | tf_op jit(solution)/shard_map/all_to_all | solution.py:99
  21.6 7.1 %collective-permute-start = (f32[1,2,5,128]{3,1,0,2:T(2,128)S(1)}, f32[1,2,5,128]{3,1,0,2:T(2,128)S(1)}, u32[]{:S(2)}, u32[]{:S(2)}) collective-permute-start(f32[1,2,5,128]{3,1,0,2:T(2,128)S(1)} %get-tuple-element.362), channel_id=1, source_target_pairs={{0,15},{1,0},{2,1},{3,2},{4,3},{5,4},{6,5},{7,6},{8,7},{9,8},{10,9... | collective-permute-start | bytes 15368 | tf_op jit(solution)/shard_map/ppermute | solution.py:20
  27.2 5.9 %collective-permute-start.1 = (f32[1,2,5,128]{3,1,0,2:T(2,128)S(1)}, f32[1,2,5,128]{3,1,0,2:T(2,128)S(1)}, u32[]{:S(2)}, u32[]{:S(2)}) collective-permute-start(f32[1,2,5,128]{3,1,0,2:T(2,128)S(1)} %get-tuple-element.361), channel_id=1, source_target_pairs={{0,14},{1,15},{2,0},{3,1},{4,2},{5,3},{6,4},{7,5},{8,6},{9,7},{10,... | collective-permute-start | bytes 15368 | tf_op jit(solution)/shard_map/ppermute | solution.py:20
  27.8 5.3 %collective-permute-start.2 = (f32[1,2,5,128]{3,1,0,2:T(2,128)S(1)}, f32[1,2,5,128]{3,1,0,2:T(2,128)S(1)}, u32[]{:S(2)}, u32[]{:S(2)}) collective-permute-start(f32[1,2,5,128]{3,1,0,2:T(2,128)S(1)} %get-tuple-element.360), channel_id=1, source_target_pairs={{0,13},{1,14},{2,15},{3,0},{4,1},{5,2},{6,3},{7,4},{8,5},{9,6},{10... | collective-permute-start | bytes 15368 | tf_op jit(solution)/shard_map/ppermute | solution.py:20
  27.9 6.7 %collective-permute-start.3 = (f32[1,2,5,128]{3,1,0,2:T(2,128)S(1)}, f32[1,2,5,128]{3,1,0,2:T(2,128)S(1)}, u32[]{:S(2)}, u32[]{:S(2)}) collective-permute-start(f32[1,2,5,128]{3,1,0,2:T(2,128)S(1)} %get-tuple-element.359), channel_id=1, source_target_pairs={{0,12},{1,13},{2,14},{3,15},{4,0},{5,1},{6,2},{7,3},{8,4},{9,5},{1... | collective-permute-start | bytes 15368 | tf_op jit(solution)/shard_map/ppermute | solution.py:20
  28.5 7.6 %collective-permute-start.4 = (f32[1,2,5,128]{3,1,0,2:T(2,128)S(1)}, f32[1,2,5,128]{3,1,0,2:T(2,128)S(1)}, u32[]{:S(2)}, u32[]{:S(2)}) collective-permute-start(f32[1,2,5,128]{3,1,0,2:T(2,128)S(1)} %get-tuple-element.358), channel_id=1, source_target_pairs={{0,11},{1,12},{2,13},{3,14},{4,15},{5,0},{6,1},{7,2},{8,3},{9,4},{... | collective-permute-start | bytes 15368 | tf_op jit(solution)/shard_map/ppermute | solution.py:20
  28.8 9.7 %collective-permute-start.5 = (f32[1,2,5,128]{3,1,0,2:T(2,128)S(1)}, f32[1,2,5,128]{3,1,0,2:T(2,128)S(1)}, u32[]{:S(2)}, u32[]{:S(2)}) collective-permute-start(f32[1,2,5,128]{3,1,0,2:T(2,128)S(1)} %get-tuple-element.357), channel_id=1, source_target_pairs={{0,10},{1,11},{2,12},{3,13},{4,14},{5,15},{6,0},{7,1},{8,2},{9,3},... | collective-permute-start | bytes 15368 | tf_op jit(solution)/shard_map/ppermute | solution.py:20
  33.1 5.5 %collective-permute-start.6 = (f32[1,2,5,128]{3,1,0,2:T(2,128)S(1)}, f32[1,2,5,128]{3,1,0,2:T(2,128)S(1)}, u32[]{:S(2)}, u32[]{:S(2)}) collective-permute-start(f32[1,2,5,128]{3,1,0,2:T(2,128)S(1)} %get-tuple-element.356), channel_id=1, source_target_pairs={{0,9},{1,10},{2,11},{3,12},{4,13},{5,14},{6,15},{7,0},{8,1},{9,2},... | collective-permute-start | bytes 15368 | tf_op jit(solution)/shard_map/ppermute | solution.py:20
  33.1 7.8 %collective-permute-start.7 = (f32[1,2,5,128]{3,1,0,2:T(2,128)S(1)}, f32[1,2,5,128]{3,1,0,2:T(2,128)S(1)}, u32[]{:S(2)}, u32[]{:S(2)}) collective-permute-start(f32[1,2,5,128]{3,1,0,2:T(2,128)S(1)} %get-tuple-element.355), channel_id=1, source_target_pairs={{0,8},{1,9},{2,10},{3,11},{4,12},{5,13},{6,14},{7,15},{8,0},{9,1},... | collective-permute-start | bytes 15368 | tf_op jit(solution)/shard_map/ppermute | solution.py:20
  34.6 8.4 %collective-permute-start.8 = (f32[1,2,5,128]{3,1,0,2:T(2,128)S(1)}, f32[1,2,5,128]{3,1,0,2:T(2,128)S(1)}, u32[]{:S(2)}, u32[]{:S(2)}) collective-permute-start(f32[1,2,5,128]{3,1,0,2:T(2,128)S(1)} %get-tuple-element.354), channel_id=1, source_target_pairs={{0,7},{1,8},{2,9},{3,10},{4,11},{5,12},{6,13},{7,14},{8,15},{9,0},... | collective-permute-start | bytes 15368 | tf_op jit(solution)/shard_map/ppermute | solution.py:20
  36.1 7.7 %collective-permute-start.9 = (f32[1,2,5,128]{3,1,0,2:T(2,128)S(1)}, f32[1,2,5,128]{3,1,0,2:T(2,128)S(1)}, u32[]{:S(2)}, u32[]{:S(2)}) collective-permute-start(f32[1,2,5,128]{3,1,0,2:T(2,128)S(1)} %get-tuple-element.353), channel_id=1, source_target_pairs={{0,6},{1,7},{2,8},{3,9},{4,10},{5,11},{6,12},{7,13},{8,14},{9,15},... | collective-permute-start | bytes 15368 | tf_op jit(solution)/shard_map/ppermute | solution.py:20
  38.5 5.4 %collective-permute-start.10 = (f32[1,2,5,128]{3,1,0,2:T(2,128)S(1)}, f32[1,2,5,128]{3,1,0,2:T(2,128)S(1)}, u32[]{:S(2)}, u32[]{:S(2)}) collective-permute-start(f32[1,2,5,128]{3,1,0,2:T(2,128)S(1)} %get-tuple-element.352), channel_id=1, source_target_pairs={{0,5},{1,6},{2,7},{3,8},{4,9},{5,10},{6,11},{7,12},{8,13},{9,14},{... | collective-permute-start | bytes 15368 | tf_op jit(solution)/shard_map/ppermute | solution.py:20
  38.6 5.4 %collective-permute-start.11 = (f32[1,2,5,128]{3,1,0,2:T(2,128)S(1)}, f32[1,2,5,128]{3,1,0,2:T(2,128)S(1)}, u32[]{:S(2)}, u32[]{:S(2)}) collective-permute-start(f32[1,2,5,128]{3,1,0,2:T(2,128)S(1)} %get-tuple-element.351), channel_id=1, source_target_pairs={{0,4},{1,5},{2,6},{3,7},{4,8},{5,9},{6,10},{7,11},{8,12},{9,13},{1... | collective-permute-start | bytes 15368 | tf_op jit(solution)/shard_map/ppermute | solution.py:20
  40.9 5.4 %collective-permute-start.12 = (f32[1,2,5,128]{3,1,0,2:T(2,128)S(1)}, f32[1,2,5,128]{3,1,0,2:T(2,128)S(1)}, u32[]{:S(2)}, u32[]{:S(2)}) collective-permute-start(f32[1,2,5,128]{3,1,0,2:T(2,128)S(1)} %get-tuple-element.350), channel_id=1, source_target_pairs={{0,3},{1,4},{2,5},{3,6},{4,7},{5,8},{6,9},{7,10},{8,11},{9,12},{10... | collective-permute-start | bytes 15368 | tf_op jit(solution)/shard_map/ppermute | solution.py:20
  43.0 6.3 %collective-permute-start.13 = (f32[1,2,5,128]{3,1,0,2:T(2,128)S(1)}, f32[1,2,5,128]{3,1,0,2:T(2,128)S(1)}, u32[]{:S(2)}, u32[]{:S(2)}) collective-permute-start(f32[1,2,5,128]{3,1,0,2:T(2,128)S(1)} %get-tuple-element.349), channel_id=1, source_target_pairs={{0,2},{1,3},{2,4},{3,5},{4,6},{5,7},{6,8},{7,9},{8,10},{9,11},{10,... | collective-permute-start | bytes 15368 | tf_op jit(solution)/shard_map/ppermute | solution.py:20
  43.8 5.7 %collective-permute-start.14 = (f32[1,2,5,128]{3,1,0,2:T(2,128)S(1)}, f32[1,2,5,128]{3,1,0,2:T(2,128)S(1)}, u32[]{:S(2)}, u32[]{:S(2)}) collective-permute-start(f32[1,2,5,128]{3,1,0,2:T(2,128)S(1)} %get-tuple-element.348), channel_id=1, source_target_pairs={{0,1},{1,2},{2,3},{3,4},{4,5},{5,6},{6,7},{7,8},{8,9},{9,10},{10,1... | collective-permute-start | bytes 15368 | tf_op jit(solution)/shard_map/ppermute | solution.py:20
  49.7 4.6 %copy-start.5 = (f32[16,128]{1,0:T(8,128)S(1)}, f32[16,128]{1,0:T(8,128)}, u32[]{:S(2)}) copy-start(f32[16,128]{1,0:T(8,128)} %param.21) | copy-start | bytes 24580
  49.7 4.6 %copy-start.7 = (f32[16,128]{1,0:T(8,128)S(1)}, f32[16,128]{1,0:T(8,128)}, u32[]{:S(2)}) copy-start(f32[16,128]{1,0:T(8,128)} %param.23) | copy-start | bytes 24580
  62.0 10.0 %all-to-all-start.1 = ((f32[16,2,128]{2,1,0:T(2,128)}), f32[16,2,128]{2,1,0:T(2,128)S(1)}, u32[]{:S(2)}, u32[]{:S(2)}) async-start(f32[16,2,128]{2,1,0:T(2,128)} %bitcast.59), calls=%async_computation.1 | async-start | bytes 32768 | tf_op jit(solution)/shard_map/all_to_all | solution.py:118
  (1 other events, 2.3 us)
